TPU v7x, 512 devices: a whole 4x8x8 slice. The times are simulated.
512 devices in a mesh: ka: 16 (over y_hi, x), band: 32 (over y_lo, z, core).
Axes of the slice: x: 4, y: 8 (y_hi: 4, y_lo: 2; y = y_hi * 2 + y_lo), z: 8, core: 2. Of those that a mesh axis runs over, the one named last changes fastest.
Arguments:
- targets: bfloat16 [16, 32, 24, 24, 128], P('ka', 'band'), may hold values from -6 to 6
- occupied: bfloat16 [16, 64, 24, 24, 128], P('ka', 'band'), may hold values from -6 to 6
- wavevectors: int32 [16, 3], replicated, may hold values from 0 to 3
- umklapp: int32 [16, 2, 3], P('ka'), may hold values from -1 to 1
- owners: int32 [16, 2, 2], P('ka'), may hold values from 0 to 31
Outputs:
- exchange: bfloat16 [16, 32, 24, 24, 128], P('ka', 'band')
All inputs are finite; a program needn't handle non-finite values.
Results may differ from a plain program's by a relative error of at most 0.017.
Values may be sent and summed in bfloat16 or wider, within the bound.
No kernel may reach another device: no remote copies, remote signals or barrier semaphores. Data moves between devices by JAX's collectives and lax.ppermute only.
A program may use at most 64 MiB of HBM per device.

v0:
```python
import math

import jax
import jax.numpy as jnp
from jax import lax
from jax.sharding import PartitionSpec as P

OCC_DEV = 2
STEPS = 2
KGRID = 4


screening_sq = 0.16
spacing = 0.25
prefactor = -0.5


def from_behind(block, axis, distance):
    devices = range(lax.axis_size(axis))
    route = [((i - distance) % len(devices), i) for i in devices]
    return lax.ppermute(block, axis, route)


def spread(block, axis, holder):
    block = jnp.where(lax.axis_index(axis) == holder, block, jnp.zeros_like(block))
    return lax.psum(block, axis)


def tables(length):
    indices = jnp.arange(length, dtype=jnp.int32)
    products = indices[:, None] * indices[None, :] % length
    angles = products.astype(jnp.float32) * (2.0 * math.pi / length)
    return (jnp.cos(angles), jnp.sin(angles))


def last_matrix(length, sign_value):
    cosine, sine_table = tables(length)
    upper_rows = jnp.concatenate([cosine, -sign_value * sine_table], axis=1)
    bottom = jnp.concatenate([sign_value * sine_table, cosine], axis=1)
    return jnp.concatenate([upper_rows, bottom], axis=0).astype(jnp.bfloat16)


def stacked_table(length):
    cosine, sine_table = tables(length)
    return jnp.concatenate([cosine, sine_table], axis=0).astype(jnp.bfloat16)


def along_axis(grid_values, spec, length, sign_value, axis_pos):
    both = jnp.einsum(spec, stacked_table(length), grid_values, preferred_element_type=jnp.float32)
    cos_part = lax.slice_in_dim(both, 0, length, axis=axis_pos)
    sin_part = lax.slice_in_dim(both, length, 2 * length, axis=axis_pos)
    half_width = both.shape[-1] // 2
    swapped = jnp.concatenate([sin_part[..., half_width:], sin_part[..., :half_width]], axis=-1)
    half_sign = jnp.concatenate(
        [jnp.ones((half_width,), jnp.float32), -jnp.ones((half_width,), jnp.float32)]
    )
    return (cos_part + sign_value * half_sign * swapped).astype(jnp.bfloat16)


def fourier(grid_values, sign_value):
    last_width = grid_values.shape[-1]
    flattened = grid_values.reshape(-1, last_width)
    moved = jnp.dot(
        flattened, last_matrix(last_width // 2, sign_value), preferred_element_type=jnp.float32
    )
    grid_values = moved.astype(jnp.bfloat16).reshape(grid_values.shape)
    grid_values = along_axis(grid_values, "vy,byzc->bvzc", grid_values.shape[1], sign_value, 1)
    grid_values = along_axis(grid_values, "vz,byzc->byvc", grid_values.shape[2], sign_value, 2)
    return grid_values


def coulomb(shift_vec, grid_x, grid_y, grid_z):
    squares = []
    for axis_pos, length in ((0, grid_x), (1, grid_y), (2, grid_z)):
        indices = jnp.arange(length, dtype=jnp.int32)
        signed = jnp.where(indices * 2 < length, indices, indices - length)
        wavenumber = (
            2.0 * math.pi / (length * spacing) * (signed.astype(jnp.float32) + shift_vec[axis_pos])
        )
        squares.append(wavenumber * wavenumber)
    square_x = jnp.concatenate([squares[0], squares[0]])
    total_sq = (
        squares[1][:, None, None]
        + squares[2][None, :, None]
        + square_x[None, None, :]
        + screening_sq
    )
    return 4.0 * math.pi / total_sq


def pair_density(visitor, resident):
    half_width = visitor.shape[-1] // 2
    visit_re = visitor[..., :half_width].astype(jnp.float32)
    visit_im = visitor[..., half_width:].astype(jnp.float32)
    res_re = resident[..., :half_width].astype(jnp.float32)
    res_im = resident[..., half_width:].astype(jnp.float32)
    real_part = visit_re * res_re + visit_im * res_im
    imag_part = visit_re * res_im - visit_im * res_re
    return jnp.concatenate([real_part, imag_part], axis=-1).astype(jnp.bfloat16)


def apply_potential(visitor, potential):
    half_width = visitor.shape[-1] // 2
    visit_re = visitor[..., :half_width].astype(jnp.float32)
    visit_im = visitor[..., half_width:].astype(jnp.float32)
    pot_re = potential[..., :half_width].astype(jnp.float32)
    pot_im = potential[..., half_width:].astype(jnp.float32)
    real_part = visit_re * pot_re - visit_im * pot_im
    imag_part = visit_re * pot_im + visit_im * pot_re
    return jnp.concatenate([real_part, imag_part], axis=-1)


def exchange_term(visitor, resident, kernel, cells):
    density = pair_density(visitor, resident)
    spectrum = fourier(density, 1.0)
    screened = (spectrum.astype(jnp.float32) * kernel * (1.0 / cells)).astype(jnp.bfloat16)
    potential = fourier(screened, -1.0)
    return apply_potential(visitor, potential)


def local(targets, occupied, wavevectors, umklapp, owners):
    resident = targets[0]
    grid_y, grid_z, last_width = (resident.shape[1], resident.shape[2], resident.shape[3])
    grid_x = last_width // 2
    cells = float(grid_x * grid_y * grid_z)
    ka_position = lax.axis_index("ka")
    k_total = lax.axis_size("ka")
    own_coords = lax.dynamic_index_in_dim(wavevectors, ka_position, 0, keepdims=False)
    accumulated = jnp.zeros(resident.shape, jnp.float32)
    visiting = occupied[0]
    for section_index in range(1, STEPS + 1):
        visit_index = (ka_position - section_index) % k_total
        visit_coords = lax.dynamic_index_in_dim(wavevectors, visit_index, 0, keepdims=False)
        shift_vec = (own_coords - visit_coords).astype(jnp.float32) / KGRID + umklapp[
            0, section_index - 1
        ].astype(jnp.float32)
        kernel = coulomb(shift_vec, grid_x, grid_y, grid_z)
        visiting = from_behind(visiting, "ka", 1)
        for slot_index in range(OCC_DEV):
            owner_band = owners[0, section_index - 1, slot_index]
            visitor = spread(visiting[slot_index], "band", owner_band)
            accumulated = accumulated + exchange_term(visitor, resident, kernel, cells)
    return (prefactor * accumulated).astype(jnp.bfloat16)[None]


def solution(mesh):
    placed = (
        P("ka", "band", None, None, None),
        P("ka", "band", None, None, None),
        P(),
        P("ka", None, None),
        P("ka", None, None),
    )
    return jax.shard_map(
        local,
        mesh=mesh,
        in_specs=placed,
        out_specs=P("ka", "band", None, None, None),
        check_vma=False,
    )
```

profile of v0, /device:TPU:1, one launch (start us, length us, event | category | flops | bytes accessed | tf_op | source)
XLA Modules:
  0.0 300.5 jit_solution(17322508381403608833)
XLA Ops:
  6.5 1.0 copy.122
  7.5 3.9 %collective-permute-start = (bf16[2,24,24,128]{3,1,2,0:T(8,128)(2,1)S(1)}, bf16[2,24,24,128]{3,1,2,0:T(8,128)(2,1)S(1)}, u32[]{:S(2)}, u32[]{:S(2)}) collective-permute-start(bf16[2,24,24,128]{3,1,2,0:T(8,128)(2,1)S(1)} %bitcast.300), channel_id=1, source_target_pairs={{480,0},{0,32},{32,64},{64,96},{96,128},{128,160},{160,192},{192,2... | collective-permute-start | bytes 884744 | tf_op jit(solution)/shard_map/ppermute | solution.py:21
  11.6 0.7 copy-done.8
  12.3 0.7 fusion.145
  15.5 0.7 copy-done.5
  16.3 0.7 copy-done.9
  17.0 0.7 fusion.146
  17.7 0.7 multiply_multiply_fusion.1
  18.4 0.7 multiply_multiply_fusion.2
  19.0 0.6 multiply_multiply_fusion
  19.7 0.6 multiply_multiply_fusion.4
  20.3 0.6 multiply_multiply_fusion.5
  21.1 0.4 collective-permute-done
  21.5 2.7 collective-permute-start.1
  24.2 0.6 multiply_multiply_fusion.3
  24.8 0.7 fusion.62
  25.6 8.4 %collective-permute-done.1 = bf16[2,24,24,128]{3,1,2,0:T(8,128)(2,1)S(1)} collective-permute-done((bf16[2,24,24,128]{3,1,2,0:T(8,128)(2,1)S(1)}, bf16[2,24,24,128]{3,1,2,0:T(8,128)(2,1)S(1)}, u32[]{:S(2)}, u32[]{:S(2)}) %collective-permute-start.1) | collective-permute-done | bytes 294944 | tf_op jit(solution)/shard_map/ppermute | solution.py:21
  33.9 0.7 fusion.60
  34.8 0.8 copy-done.4
  35.9 237.7 %all-reduce.3.cloned.1.call-done = (bf16[24,24,128]{2,0,1:T(8,128)(2,1)}, bf16[24,24,128]{2,0,1:T(8,128)(2,1)}, bf16[24,24,128]{2,0,1:T(8,128)(2,1)}, bf16[24,24,128]{2,0,1:T(8,128)(2,1)}) async-done(((bf16[24,24,128]{2,0,1:T(8,128)(2,1)}, bf16[24,24,128]{2,0,1:T(8,128)(2,1)}, bf16[24,24,128]{2,0,1:T(8,128)(2,1)}, bf16[24,24,128]{2,0,1:T(8,128)(2,1)}), (bf16[24,24,128]{2,0,1:T(8,128)(2,1)}, ...) | async-done | bytes 589840 | tf_op jit(solution)/shard_map/psum | solution.py:26
  273.6 1.4 fusion.21
  275.4 0.3 convolution_bitcast_fusion.5
  276.1 0.3 convolution_bitcast_fusion.7
  276.6 0.7 copy-done.1
  277.4 0.3 fusion.29
  278.0 0.3 convolution_bitcast_fusion.3
  278.7 0.3 convolution_bitcast_fusion.1
  279.2 0.6 copy-done.7
  280.1 0.3 fusion.85
  280.7 0.3 fusion.79
  281.3 0.5 multiply_convert_fusion
  281.8 0.3 fusion.91
  282.4 0.3 fusion.97
  283.1 0.3 multiply_convert_fusion.2
  283.7 0.3 convolution_bitcast_fusion.6
  284.4 0.3 convolution_bitcast_fusion
  284.8 0.6 copy-done.6
  285.7 0.3 fusion.94
  286.3 0.3 fusion.76
  287.3 0.3 convolution_bitcast_fusion.4
  288.0 0.3 convolution_bitcast_fusion.2
  288.4 0.4 fusion.32
  288.8 0.3 fusion.82
  289.4 0.3 fusion.88
  290.5 0.7 copy-done.2
  291.7 0.7 copy-done
  292.6 0.4 fusion.51
  292.9 0.7 copy.71
  (75 shorter events, 8.8 us)
Async XLA Ops:
  6.5 267.1 %all-reduce.3.cloned.1.call-start = ((), (), s32[]{:S(2)}) async-start(), calls=%async_computation | async-start | bytes 1179648 | tf_op jit(solution)/shard_map/psum | solution.py:26
  7.5 13.9 %collective-permute-start = (bf16[2,24,24,128]{3,1,2,0:T(8,128)(2,1)S(1)}, bf16[2,24,24,128]{3,1,2,0:T(8,128)(2,1)S(1)}, u32[]{:S(2)}, u32[]{:S(2)}) collective-permute-start(bf16[2,24,24,128]{3,1,2,0:T(8,128)(2,1)S(1)} %bitcast.300), channel_id=1, source_target_pairs={{480,0},{0,32},{32,64},{64,96},{96,128},{128,160},{160,192},{192,2... | collective-permute-start | bytes 884744 | tf_op jit(solution)/shard_map/ppermute | solution.py:21
  11.6 0.7 copy-start.8
  15.4 0.7 copy-start.5
  16.3 0.7 copy-start.9
  21.5 12.5 %collective-permute-start.1 = (bf16[2,24,24,128]{3,1,2,0:T(8,128)(2,1)S(1)}, bf16[2,24,24,128]{3,1,2,0:T(8,128)(2,1)S(1)}, u32[]{:S(2)}, u32[]{:S(2)}) collective-permute-start(bf16[2,24,24,128]{3,1,2,0:T(8,128)(2,1)S(1)} %collective-permute-done), channel_id=1, source_target_pairs={{480,0},{0,32},{32,64},{64,96},{96,128},{128,160},{160,192},{192,2... | collective-permute-start | bytes 884744 | tf_op jit(solution)/shard_map/ppermute | solution.py:21
  34.7 0.9 copy-start.4
  276.4 0.9 copy-start.1
  276.4 1.0 copy-start.3
  279.2 0.7 copy-start.7
  284.8 0.7 copy-start.6
  290.3 0.9 copy-start.2
  291.4 0.9 copy-start
Sparse Core Ops, SparseCore 0:
  34.8 238.7 all-reduce.2
where the time goes:
time: 302 us; the launch traced here: 300 us
  waiting for transfers between devices  246 us (81%)
  between operations  16.6 us (5%)
  local copies, waits for them, and re-layouts  13.4 us (4%)
  other arithmetic  11 us (4%)
  starting transfers between devices  6.66 us (2%)
  matrix products  6.39 us (2%)
    psum x1, waiting for transfers between devices, spread(): return lax.psum(block, axis)  238 us
    ppermute x2, waiting for transfers between devices, from_behind(): return lax.ppermute(block, axis, route)  8.77 us
    unnamed x22, local copies, waits for them, and re-layouts  7.33 us
    ppermute x2, starting transfers between devices, from_behind(): return lax.ppermute(block, axis, route)  6.66 us
  transfers between devices with their start and end apart: 3, of which 3 were waited for; matrix products, arithmetic and copies ran while one was open for 2% of the time, Pallas kernels for 0%

commit v1 on v0

v1 whole, which is shorter than its diff:
```python
import math

import jax
import jax.numpy as jnp
import ml_dtypes
import numpy as np
from jax import lax
from jax.experimental import pallas as pl
from jax.experimental.pallas import tpu as pltpu
from jax.sharding import PartitionSpec as P

OCC_DEV = 2
STEPS = 2
KGRID = 4

screening_sq = 0.16
spacing = 0.25
prefactor = -0.5

PIECE = 40
PIECES = 16
LANES = 128


def shift_ka(block, distance):
    size = lax.axis_size("ka")
    return lax.ppermute(block, "ka", [(i, (i + distance) % size) for i in range(size)])


def band_groups():
    along_z = [[y * 16 + z * 2 + c for z in range(8)] for y in range(2) for c in range(2)]
    along_yc = [[y * 16 + z * 2 + c for y in range(2) for c in range(2)] for z in range(8)]
    return along_z, along_yc


def rounded_tables(length):
    indices = np.arange(length)
    angles = (indices[:, None] * indices[None, :] % length) * (2.0 * math.pi / length)
    rounded = lambda t: t.astype(np.float32).astype(ml_dtypes.bfloat16).astype(np.float64)
    return rounded(np.cos(angles)), rounded(np.sin(angles))


def plane_table(grid_y, grid_z):
    cos_y, sin_y = rounded_tables(grid_y)
    cos_z, sin_z = rounded_tables(grid_z)
    cosine = np.kron(cos_y, cos_z) - np.kron(sin_y, sin_z)
    sine = np.kron(sin_y, cos_z) + np.kron(cos_y, sin_z)
    return np.concatenate([cosine, sine], axis=1).astype(np.float32).astype(ml_dtypes.bfloat16)


def line_table(grid_x, sign):
    cosine, sine = rounded_tables(grid_x)
    re_in = np.concatenate([cosine, -sign * sine], axis=1)
    im_in = np.concatenate([sign * sine, cosine], axis=1)
    straight = np.concatenate([re_in, im_in], axis=0)
    turned = np.concatenate([sign * straight[:, grid_x:], -sign * straight[:, :grid_x]], axis=1)
    return np.concatenate([straight, turned], axis=1).astype(np.float32).astype(ml_dtypes.bfloat16)


def coulomb(shift_vec, grid_x, grid_y, grid_z):
    squares = []
    for axis_pos, length in ((0, grid_x), (1, grid_y), (2, grid_z)):
        indices = jnp.arange(length, dtype=jnp.int32)
        signed = jnp.where(indices * 2 < length, indices, indices - length)
        wavenumber = (
            2.0 * math.pi / (length * spacing) * (signed.astype(jnp.float32) + shift_vec[axis_pos])
        )
        squares.append(wavenumber * wavenumber)
    square_x = jnp.concatenate([squares[0], squares[0]])
    total_sq = (
        squares[1][:, None, None]
        + squares[2][None, :, None]
        + square_x[None, None, :]
        + screening_sq
    )
    return 4.0 * math.pi / total_sq


def exchange_kernel(pieces, psi, table, forward, inverse, kern, out, direct, cross, stack):
    rows, half = out.shape[0], LANES // 2
    terms = STEPS * OCC_DEV
    left = lax.broadcasted_iota(jnp.int32, (1, LANES), 1) < half

    for piece in range(PIECES):
        first = piece * PIECE
        count = min(PIECE, rows - first)
        if count <= 0:
            continue
        own = psi[pl.ds(first, count), :].astype(jnp.float32)
        own_turned = pltpu.roll(own, half, 1)
        for term in range(terms):
            s, r = divmod(term, OCC_DEV)
            z, c = divmod(piece, 2)
            phi = pieces[r * 2 + c, z, s].astype(jnp.float32)[:count]
            phi_turned = pltpu.roll(phi, half, 1)
            a = jnp.where(left, phi, phi_turned)
            b = jnp.where(left, -phi_turned, phi)
            direct[term, pl.ds(first, count), :] = a
            cross[term, pl.ds(first, count), :] = b
            density = (a * own - b * own_turned).astype(jnp.bfloat16)
            both = jnp.dot(density, forward[...], preferred_element_type=jnp.float32)
            lane = term * LANES
            stack[pl.ds(first, count), pl.ds(lane, LANES)] = both[:, :LANES]
            stack[pl.ds(rows + first, count), pl.ds(lane, LANES)] = both[:, LANES:]

    spectrum = jnp.dot(
        table[...], stack[...].astype(jnp.bfloat16), preferred_element_type=jnp.float32
    )
    for term in range(terms):
        lane = term * LANES
        screened = (spectrum[:, lane : lane + LANES] * kern[term // OCC_DEV]).astype(jnp.bfloat16)
        both = jnp.dot(screened, inverse[...], preferred_element_type=jnp.float32)
        stack[pl.ds(0, rows), pl.ds(lane, LANES)] = both[:, :LANES]
        stack[pl.ds(rows, rows), pl.ds(lane, LANES)] = both[:, LANES:]
    potential = jnp.dot(
        table[...], stack[...].astype(jnp.bfloat16), preferred_element_type=jnp.float32
    )
    total = jnp.zeros((rows, LANES), jnp.float32)
    for term in range(terms):
        lane = term * LANES
        pot = potential[:, lane : lane + LANES]
        total += direct[term] * pot + cross[term] * pltpu.roll(pot, half, 1)
    out[...] = (prefactor * total).astype(out.dtype)


def apply_exchange(pieces, psi, kern, grid_x, grid_y, grid_z):
    rows = grid_y * grid_z
    terms = STEPS * OCC_DEV
    vmem = pl.BlockSpec(memory_space=pltpu.VMEM)
    return pl.pallas_call(
        exchange_kernel,
        out_shape=jax.ShapeDtypeStruct((rows, LANES), jnp.bfloat16),
        in_specs=[vmem] * 6,
        out_specs=vmem,
        scratch_shapes=[
            pltpu.VMEM((terms, rows, LANES), jnp.float32),
            pltpu.VMEM((terms, rows, LANES), jnp.float32),
            pltpu.VMEM((2 * rows, terms * LANES), jnp.float32),
        ],
        compiler_params=pltpu.CompilerParams(vmem_limit_bytes=40 * 1024 * 1024),
    )(
        pieces,
        psi,
        jnp.asarray(plane_table(grid_y, grid_z)),
        jnp.asarray(line_table(grid_x, 1.0)),
        jnp.asarray(line_table(grid_x, -1.0)),
        kern,
    )


def local(targets, occupied, wavevectors, umklapp, owners):
    resident = targets[0, 0]
    grid_y, grid_z, last_width = resident.shape
    grid_x = last_width // 2
    rows = grid_y * grid_z
    cells = float(grid_x * rows)
    ka_position = lax.axis_index("ka")
    k_total = lax.axis_size("ka")
    slot = lax.axis_index("band") // PIECES
    along_z, along_yc = band_groups()

    wanted = [shift_ka(owners[0, s - 1], -s) for s in range(1, STEPS + 1)]

    flat = occupied[0].reshape(OCC_DEV, rows, last_width)
    flat = jnp.pad(flat, ((0, 0), (0, PIECE * PIECES - rows), (0, 0)))
    flat = flat.reshape(OCC_DEV * PIECES, PIECE, last_width)
    spread = lax.all_to_all(flat, "band", 0, 0, tiled=True)

    chosen = []
    for s in range(1, STEPS + 1):
        owner = lax.dynamic_index_in_dim(wanted[s - 1], slot, 0, keepdims=False)
        piece = lax.dynamic_index_in_dim(spread, owner, 0, keepdims=False)
        chosen.append(shift_ka(piece, s))
    mine = jnp.stack(chosen)

    column = jnp.broadcast_to(mine[None], (8,) + mine.shape)
    column = lax.all_to_all(column, "band", 0, 0, tiled=True, axis_index_groups=along_z)
    pieces = lax.all_gather(column, "band", axis_index_groups=along_yc)

    own_coords = lax.dynamic_index_in_dim(wavevectors, ka_position, 0, keepdims=False)
    kernels = []
    for s in range(1, STEPS + 1):
        visit_coords = lax.dynamic_index_in_dim(
            wavevectors, (ka_position - s) % k_total, 0, keepdims=False
        )
        shift_vec = (own_coords - visit_coords).astype(jnp.float32) / KGRID + umklapp[
            0, s - 1
        ].astype(jnp.float32)
        kernels.append(coulomb(shift_vec, grid_x, grid_y, grid_z) * (1.0 / cells))
    kern = jnp.stack(kernels).reshape(STEPS, rows, last_width)

    result = apply_exchange(
        pieces, resident.reshape(rows, last_width), kern, grid_x, grid_y, grid_z
    )
    return result.reshape((1, 1) + resident.shape)


def solution(mesh):
    placed = (
        P("ka", "band", None, None, None),
        P("ka", "band", None, None, None),
        P(),
        P("ka", None, None),
        P("ka", None, None),
    )
    return jax.shard_map(
        local,
        mesh=mesh,
        in_specs=placed,
        out_specs=P("ka", "band", None, None, None),
        check_vma=False,
    )
```

time: 302 us -> 78.6 us (0.26)
  waiting for transfers between devices: 246 us -> 14.4 us
  starting transfers between devices: 6.66 us -> 34.7 us
  between operations: 16.6 us -> 4.23 us
  blocking collectives: 0 us -> 10.9 us
  local copies, waits for them, and re-layouts: 13.4 us -> 5.61 us
  matrix products: 6.39 us -> 0 us
  other arithmetic: 11 us -> 4.72 us
  Pallas kernels: 0 us -> 3.49 us
    psum x1 -> x0, waiting for transfers between devices: 238 us -> none  [spread(): return lax.psum(block, axis)]
    all_to_all x0 -> x2, starting transfers between devices: none -> 17.1 us  [the longest x1 11.8 us: local(): spread = lax.all_to_all(flat, 'band', 0, 0, tiled=True)]
    all_gather x0 -> x1, blocking collectives: none -> 10.9 us  [local(): pieces = lax.all_gather(column, 'band', axis_index_groups=along_yc)]
    ppermute x2 -> x4, starting transfers between devices: 6.66 us -> 17.6 us  [shift_ka(): lax.ppermute(block, 'ka', [(i, (i + distance) % size) for i in range(size)])]
    all_to_all x0 -> x2, waiting for transfers between devices: none -> 9.6 us  [the longest x1 8.15 us: local(): lax.all_to_all(column, 'band', 0, 0, tiled=True, axis_index_groups=along_z)]
    unnamed x22 -> x12, local copies, waits for them, and re-layouts: 7.33 us -> 0.02 us
    dot_general x24 -> x0, matrix products: 6.39 us -> none  [the longest x16 4.37 us: along_axis(): jnp.einsum(spec, stacked_table(length), grid_values, preferred_element_ty...]
    ppermute x2 -> x4, waiting for transfers between devices: 8.77 us -> 4.83 us  [shift_ka(): lax.ppermute(block, 'ka', [(i, (i + distance) % size) for i in range(size)])]
  transfers between devices with their start and end apart: 3 -> 6, of which waited for: 3 -> 4; matrix products, arithmetic and copies ran while one was open for 2% -> 11% of each run, Pallas kernels for 0% -> 0%
where the time goes in v1:
time: 78.6 us; the launch traced here: 78.1 us
  starting transfers between devices  34.7 us (44%)
  waiting for transfers between devices  14.4 us (18%)
  blocking collectives  10.9 us (14%)
  local copies, waits for them, and re-layouts  5.61 us (7%)
  other arithmetic  4.72 us (6%)
  between operations  4.23 us (5%)
  Pallas kernels  3.49 us (4%)
    ppermute x4, starting transfers between devices, shift_ka(): lax.ppermute(block, 'ka', [(i, (i + distance) % size) for i in range(size)])  17.6 us
    all_to_all x1, starting transfers between devices, local(): spread = lax.all_to_all(flat, 'band', 0, 0, tiled=True)  11.8 us
    all_gather x1, blocking collectives, local(): pieces = lax.all_gather(column, 'band', axis_index_groups=along_yc)  10.9 us
    all_to_all x1, waiting for transfers between devices, local(): lax.all_to_all(column, 'band', 0, 0, tiled=True, axis_index_groups=along_z)  8.15 us
    all_to_all x1, starting transfers between devices, local(): lax.all_to_all(column, 'band', 0, 0, tiled=True, axis_index_groups=along_z)  5.28 us
    ppermute x4, waiting for transfers between devices, shift_ka(): lax.ppermute(block, 'ka', [(i, (i + distance) % size) for i in range(size)])  4.83 us
    mul x6, other arithmetic, coulomb(): squares.append(wavenumber * wavenumber)  3.98 us
    pallas_call x1, Pallas kernels, apply_exchange(): pl.pallas_call(exchange_kernel, out_shape=jax.ShapeDtypeStruct((rows, LAN...  3.49 us
  transfers between devices with their start and end apart: 6, of which 4 were waited for; matrix products, arithmetic and copies ran while one was open for 11% of the time, Pallas kernels for 0%

profile of v1, /device:TPU:1, one launch (start us, length us, event | category | flops | bytes accessed | tf_op | source)
XLA Modules:
  0.0 78.1 jit_solution(16137722586153293302)
XLA Ops:
  0.0 0.0 copy-start.4
  0.0 0.0 copy-start.5
  0.0 0.8 slice_bitcast_fusion.1
  0.8 8.9 %collective-permute-start = (s32[2]{0:T(128)S(1)}, s32[2]{0:T(128)S(1)}, u32[]{:S(2)}, u32[]{:S(2)}) collective-permute-start(s32[2]{0:T(128)S(1)} %get-tuple-element.11), channel_id=1, source_target_pairs={{0,480},{32,0},{64,32},{96,64},{128,96},{160,128},{192,160},{224,1... | collective-permute-start | bytes 32 | tf_op jit(solution)/shard_map/ppermute | solution.py:27
  9.7 2.4 %collective-permute-start.2 = (s32[2]{0:T(128)S(1)}, s32[2]{0:T(128)S(1)}, u32[]{:S(2)}, u32[]{:S(2)}) collective-permute-start(s32[2]{0:T(128)S(1)} %get-tuple-element.12), channel_id=1, source_target_pairs={{0,448},{32,480},{64,0},{96,32},{128,64},{160,96},{192,128},{224,1... | collective-permute-start | bytes 32 | tf_op jit(solution)/shard_map/ppermute | solution.py:27
  12.1 1.7 %pad.4 = bf16[2,640,128]{2,1,0:T(8,128)(2,1)} pad(bf16[2,576,128]{2,1,0:T(8,128)(2,1)} %bitcast.29, bf16[]{:T(256)} %constant.76.clone.1), padding=0_0x0_64x0_0 | pad | bytes 622594 | tf_op jit(solution)/shard_map/jit(_pad)/pad | solution.py:165
  13.8 11.8 %all-to-all-start = ((bf16[32,40,128]{2,1,0:T(8,128)(2,1)}), bf16[32,40,128]{2,1,0:T(8,128)(2,1)S(1)}, u32[]{:S(2)}, u32[]{:S(2)}) async-start(bf16[32,40,128]{2,1,0:T(8,128)(2,1)} %bitcast.1), calls=%async_computation | async-start | bytes 655360 | tf_op jit(solution)/shard_map/all_to_all | solution.py:167
  25.7 0.0 copy-done.4
  25.7 0.2 multiply_reduce_fusion.1
  25.9 0.0 copy-done.5
  25.9 0.7 fusion.2
  26.6 0.7 multiply_multiply_fusion.4
  27.3 0.7 multiply_multiply_fusion.3
  27.9 0.1 pad_maximum_fusion.2
  28.0 0.7 multiply_multiply_fusion.5
  28.7 0.1 add.225
  28.8 0.1 add.226
  28.9 0.1 add.230
  29.0 0.6 multiply_multiply_fusion.2
  29.6 0.6 multiply_multiply_fusion
  30.3 0.7 multiply_multiply_fusion.1
  31.0 0.2 divide_multiply_fusion.1
  31.2 0.0 collective-permute-done
  31.2 0.6 dynamic_slice.24
  33.1 0.0 collective-permute-done.2
  33.1 0.7 dynamic_slice.26
  36.4 1.4 %all-to-all-done = bf16[32,40,128]{2,1,0:T(8,128)(2,1)S(1)} async-done(((bf16[32,40,128]{2,1,0:T(8,128)(2,1)}), bf16[32,40,128]{2,1,0:T(8,128)(2,1)S(1)}, u32[]{:S(2)}, u32[]{:S(2)}) %all-to-all-start) | async-done | bytes 327712 | tf_op jit(solution)/shard_map/all_to_all | solution.py:167
  37.8 2.5 %collective-permute-start.1 = (bf16[40,128]{1,0:T(8,128)(2,1)S(1)}, bf16[40,128]{1,0:T(8,128)(2,1)S(1)}, u32[]{:S(2)}, u32[]{:S(2)}) collective-permute-start(bf16[40,128]{1,0:T(8,128)(2,1)S(1)} %get-tuple-element.7), channel_id=1, source_target_pairs={{0,32},{32,64},{64,96},{96,128},{128,160},{160,192},{192,224},{224... | collective-permute-start | bytes 30728 | tf_op jit(solution)/shard_map/ppermute | solution.py:27
  40.4 3.8 %collective-permute-start.3 = (bf16[40,128]{1,0:T(8,128)(2,1)S(1)}, bf16[40,128]{1,0:T(8,128)(2,1)S(1)}, u32[]{:S(2)}, u32[]{:S(2)}) collective-permute-start(bf16[40,128]{1,0:T(8,128)(2,1)S(1)} %get-tuple-element.8), channel_id=1, source_target_pairs={{0,64},{32,96},{64,128},{96,160},{128,192},{160,224},{192,256},{22... | collective-permute-start | bytes 30728 | tf_op jit(solution)/shard_map/ppermute | solution.py:27
  44.1 0.1 pad_maximum_fusion.3
  44.2 0.1 add.248
  44.3 0.1 add.243
  44.4 0.1 add.244
  44.5 2.0 %collective-permute-done.1 = bf16[40,128]{1,0:T(8,128)(2,1)S(1)} collective-permute-done((bf16[40,128]{1,0:T(8,128)(2,1)S(1)}, bf16[40,128]{1,0:T(8,128)(2,1)S(1)}, u32[]{:S(2)}, u32[]{:S(2)}) %collective-permute-start.1) | collective-permute-done | bytes 10272 | tf_op jit(solution)/shard_map/ppermute | solution.py:27
  46.5 2.8 %collective-permute-done.3 = bf16[40,128]{1,0:T(8,128)(2,1)S(1)} collective-permute-done((bf16[40,128]{1,0:T(8,128)(2,1)S(1)}, bf16[40,128]{1,0:T(8,128)(2,1)S(1)}, u32[]{:S(2)}, u32[]{:S(2)}) %collective-permute-start.3) | collective-permute-done | bytes 10272 | tf_op jit(solution)/shard_map/ppermute | solution.py:27
  49.3 0.7 broadcast_in_dim.2
  50.0 0.0 copy-start
  50.0 0.0 copy-start.1
  50.0 5.3 %all-to-all-start.1 = ((bf16[8,2,40,128]{3,2,1,0:T(8,128)(2,1)}), bf16[8,2,40,128]{3,2,1,0:T(8,128)(2,1)S(1)}, u32[]{:S(2)}, u32[]{:S(2)}) async-start(bf16[8,2,40,128]{3,2,1,0:T(8,128)(2,1)} %broadcast_in_dim.2), calls=%async_computation.1 | async-start | bytes 327680 | tf_op jit(solution)/shard_map/all_to_all | solution.py:177
  55.3 0.1 divide_multiply_fusion
  55.4 0.1 pad_maximum_fusion.kern
  55.5 8.2 %all-to-all-done.1 = bf16[8,2,40,128]{3,2,1,0:T(8,128)(2,1)S(1)} async-done(((bf16[8,2,40,128]{3,2,1,0:T(8,128)(2,1)}), bf16[8,2,40,128]{3,2,1,0:T(8,128)(2,1)S(1)}, u32[]{:S(2)}, u32[]{:S(2)}) %all-to-all-start.1) | async-done | bytes 163872 | tf_op jit(solution)/shard_map/all_to_all | solution.py:177
  63.6 10.9 %all-gather = bf16[32,2,40,128]{3,2,1,0:T(8,128)(2,1)S(1)} all-gather(bf16[8,2,40,128]{3,2,1,0:T(8,128)(2,1)S(1)} %all-to-all-done.1), channel_id=2, replica_groups={{0,1,16,17},{2,3,18,19},{4,5,20,21},{6,7,22,23},{8,9,24,25},{10,11,26,2..., dimensions={0}, use_global_device_ids=true | all-gather | bytes 819200 | tf_op jit(solution)/shard_map/all_gather | solution.py:178
  74.6 0.0 copy-done
  74.6 0.0 copy-done.1
  74.6 0.0 copy-done.2
  74.6 0.0 copy-done.3
  74.6 3.5 %shard_map.82 = bf16[576,128]{1,0:T(8,128)(2,1)} custom-call(bf16[4,8,2,40,128]{4,3,2,1,0:T(8,128)(2,1)S(1)} %bitcast.27, bf16[576,128]{1,0:T(8,128)(2,1)S(1)} %bitcast.28, bf16[576,1152]{1,0:T(8,128)(2,1)S(1)} %copy-done, bf16[128,256]{1,0:T(8,128)(2,1)S(1)} %copy-done.3, bf16[128,256]{1,0:T(8,128)(2,1)S(1)} %copy-done.2, ...), custom_call_target="tpu_custom_call" | custom-call | tf_op jit(solution)/shard_map/pallas_call | solution.py:130
  (9 shorter events, 0.1 us)
Async XLA Ops:
  0.0 25.7 %copy-start.4 = (s32[16,3]{0,1:T(4,128)S(1)}, s32[16,3]{0,1:T(4,128)}, u32[]{:S(2)}) copy-start(s32[16,3]{0,1:T(4,128)} %param.10) | copy-start | bytes 580
  0.0 25.9 %copy-start.5 = (s32[1,2,3]{2,1,0:T(2,128)S(1)}, s32[1,2,3]{2,1,0:T(2,128)}, u32[]{:S(2)}) copy-start(s32[1,2,3]{2,1,0:T(2,128)} %param.11) | copy-start | bytes 76
  0.8 30.4 %collective-permute-start = (s32[2]{0:T(128)S(1)}, s32[2]{0:T(128)S(1)}, u32[]{:S(2)}, u32[]{:S(2)}) collective-permute-start(s32[2]{0:T(128)S(1)} %get-tuple-element.11), channel_id=1, source_target_pairs={{0,480},{32,0},{64,32},{96,64},{128,96},{160,128},{192,160},{224,1... | collective-permute-start | bytes 32 | tf_op jit(solution)/shard_map/ppermute | solution.py:27
  9.7 23.4 %collective-permute-start.2 = (s32[2]{0:T(128)S(1)}, s32[2]{0:T(128)S(1)}, u32[]{:S(2)}, u32[]{:S(2)}) collective-permute-start(s32[2]{0:T(128)S(1)} %get-tuple-element.12), channel_id=1, source_target_pairs={{0,448},{32,480},{64,0},{96,32},{128,64},{160,96},{192,128},{224,1... | collective-permute-start | bytes 32 | tf_op jit(solution)/shard_map/ppermute | solution.py:27
  13.8 24.0 %all-to-all-start = ((bf16[32,40,128]{2,1,0:T(8,128)(2,1)}), bf16[32,40,128]{2,1,0:T(8,128)(2,1)S(1)}, u32[]{:S(2)}, u32[]{:S(2)}) async-start(bf16[32,40,128]{2,1,0:T(8,128)(2,1)} %bitcast.1), calls=%async_computation | async-start | bytes 655360 | tf_op jit(solution)/shard_map/all_to_all | solution.py:167
  37.8 8.6 %collective-permute-start.1 = (bf16[40,128]{1,0:T(8,128)(2,1)S(1)}, bf16[40,128]{1,0:T(8,128)(2,1)S(1)}, u32[]{:S(2)}, u32[]{:S(2)}) collective-permute-start(bf16[40,128]{1,0:T(8,128)(2,1)S(1)} %get-tuple-element.7), channel_id=1, source_target_pairs={{0,32},{32,64},{64,96},{96,128},{128,160},{160,192},{192,224},{224... | collective-permute-start | bytes 30728 | tf_op jit(solution)/shard_map/ppermute | solution.py:27
  40.4 8.9 %collective-permute-start.3 = (bf16[40,128]{1,0:T(8,128)(2,1)S(1)}, bf16[40,128]{1,0:T(8,128)(2,1)S(1)}, u32[]{:S(2)}, u32[]{:S(2)}) collective-permute-start(bf16[40,128]{1,0:T(8,128)(2,1)S(1)} %get-tuple-element.8), channel_id=1, source_target_pairs={{0,64},{32,96},{64,128},{96,160},{128,192},{160,224},{192,256},{22... | collective-permute-start | bytes 30728 | tf_op jit(solution)/shard_map/ppermute | solution.py:27
  50.0 24.6 %copy-start = (bf16[576,1152]{1,0:T(8,128)(2,1)S(1)}, bf16[576,1152]{1,0:T(8,128)(2,1)}, u32[]{:S(2)}) copy-start(bf16[576,1152]{1,0:T(8,128)(2,1)} %constant.99.clone.table) | copy-start | bytes 3981316
  50.0 24.6 %copy-start.1 = (bf16[1,1,24,24,128]{4,3,2,1,0:T(8,128)(2,1)S(1)}, bf16[1,1,24,24,128]{4,3,2,1,0:T(8,128)(2,1)}, u32[]{:S(2)}) copy-start(bf16[1,1,24,24,128]{4,3,2,1,0:T(8,128)(2,1)} %param.8) | copy-start | bytes 442372
  50.0 24.6 %copy-start.2 = (bf16[128,256]{1,0:T(8,128)(2,1)S(1)}, bf16[128,256]{1,0:T(8,128)(2,1)}, u32[]{:S(2)}) copy-start(bf16[128,256]{1,0:T(8,128)(2,1)} %constant.101.clone.inverse) | copy-start | bytes 196612
  50.0 24.6 %copy-start.3 = (bf16[128,256]{1,0:T(8,128)(2,1)S(1)}, bf16[128,256]{1,0:T(8,128)(2,1)}, u32[]{:S(2)}) copy-start(bf16[128,256]{1,0:T(8,128)(2,1)} %constant.100.clone.forward) | copy-start | bytes 196612
  50.0 13.7 %all-to-all-start.1 = ((bf16[8,2,40,128]{3,2,1,0:T(8,128)(2,1)}), bf16[8,2,40,128]{3,2,1,0:T(8,128)(2,1)S(1)}, u32[]{:S(2)}, u32[]{:S(2)}) async-start(bf16[8,2,40,128]{3,2,1,0:T(8,128)(2,1)} %broadcast_in_dim.2), calls=%async_computation.1 | async-start | bytes 327680 | tf_op jit(solution)/shard_map/all_to_all | solution.py:177

commit v2 on v1

v2 whole, which is shorter than its diff:
```python
import math

import jax
import jax.numpy as jnp
import ml_dtypes
import numpy as np
from jax import lax
from jax.experimental import pallas as pl
from jax.experimental.pallas import tpu as pltpu
from jax.sharding import PartitionSpec as P


OCC_DEV = 2
STEPS = 2
KGRID = 4

screening_sq = 0.16
spacing = 0.25
prefactor = -0.5

LANES = 128


def shift_ka_by_core(block, sign):
    n_ka, n_band = lax.axis_size("ka"), lax.axis_size("band")
    route = []
    for k in range(n_ka):
        for b in range(n_band):
            to = (k + sign * (1 + b % 2)) % n_ka
            route.append((k * n_band + b, to * n_band + b))
    return lax.ppermute(block, ("ka", "band"), route)


def band_groups():
    along_yz = [[yz * 2 + c for yz in range(16)] for c in range(2)]
    cores = [[yz * 2 + c for c in range(2)] for yz in range(16)]
    return along_yz, cores


def rounded_tables(length):
    indices = np.arange(length)
    angles = (indices[:, None] * indices[None, :] % length) * (2.0 * math.pi / length)
    rounded = lambda t: t.astype(np.float32).astype(ml_dtypes.bfloat16).astype(np.float64)
    return rounded(np.cos(angles)), rounded(np.sin(angles))


def plane_table(grid_y, grid_z):
    cos_y, sin_y = rounded_tables(grid_y)
    cos_z, sin_z = rounded_tables(grid_z)
    cosine = np.kron(cos_y, cos_z) - np.kron(sin_y, sin_z)
    sine = np.kron(sin_y, cos_z) + np.kron(cos_y, sin_z)
    return np.concatenate([cosine, sine], axis=1).astype(np.float32).astype(ml_dtypes.bfloat16)


def line_table(grid_x, sign):
    cosine, sine = rounded_tables(grid_x)
    re_in = np.concatenate([cosine, -sign * sine], axis=1)
    im_in = np.concatenate([sign * sine, cosine], axis=1)
    straight = np.concatenate([re_in, im_in], axis=0)
    turned = np.concatenate([sign * straight[:, grid_x:], -sign * straight[:, :grid_x]], axis=1)
    return np.concatenate([straight, turned], axis=1).astype(np.float32).astype(ml_dtypes.bfloat16)


def coulomb_kernel(wavevectors, umklapp, out):
    steps, grid_y, grid_z, width = out.shape
    grid_x = width // 2
    cells = float(grid_x * grid_y * grid_z)
    k = lax.axis_index("ka")
    k_total = lax.axis_size("ka")

    def square(index, length, shift):
        signed = jnp.where(index * 2 < length, index, index - length).astype(jnp.float32)
        wavenumber = 2.0 * math.pi / (length * spacing) * (signed + shift)
        return wavenumber * wavenumber

    lane = lax.broadcasted_iota(jnp.int32, (grid_z, width), 1)
    index_x = jnp.where(lane < grid_x, lane, lane - grid_x)
    index_z = lax.broadcasted_iota(jnp.int32, (grid_z, width), 0)
    for s in range(steps):
        visit = lax.rem(k + (k_total - s - 1), k_total)
        shift = [
            (wavevectors[k, a] - wavevectors[visit, a]).astype(jnp.float32) / KGRID
            + umklapp[0, s, a].astype(jnp.float32)
            for a in range(3)
        ]
        plane = square(index_x, grid_x, shift[0]) + square(index_z, grid_z, shift[2])
        plane = plane + screening_sq
        for y in range(grid_y):
            signed_y = float(y if 2 * y < grid_y else y - grid_y)
            wave_y = 2.0 * math.pi / (grid_y * spacing) * (signed_y + shift[1])
            out[s, y] = (4.0 * math.pi / cells) / (plane + wave_y * wave_y)


def coulomb(wavevectors, umklapp, grid_x, grid_y, grid_z):
    smem = pl.BlockSpec(memory_space=pltpu.SMEM)
    return pl.pallas_call(
        coulomb_kernel,
        out_shape=jax.ShapeDtypeStruct((STEPS, grid_y, grid_z, 2 * grid_x), jnp.float32),
        in_specs=[smem, smem],
        out_specs=pl.BlockSpec(memory_space=pltpu.VMEM),
    )(wavevectors, umklapp)


def exchange_kernel(visitors, psi, table, forward, inverse, kern, out, direct, cross, stack):
    rows, half = out.shape[0], LANES // 2
    terms = STEPS * OCC_DEV
    left = lax.broadcasted_iota(jnp.int32, (1, LANES), 1) < half

    chunk = 144
    for term in range(terms):
        lane = term * LANES
        for first in range(0, rows, chunk):
            own = psi[pl.ds(first, chunk), :].astype(jnp.float32)
            own_turned = pltpu.roll(own, half, 1)
            phi = visitors[term, pl.ds(first, chunk), :].astype(jnp.float32)
            phi_turned = pltpu.roll(phi, half, 1)
            a = jnp.where(left, phi, phi_turned)
            b = jnp.where(left, -phi_turned, phi)
            direct[term, pl.ds(first, chunk), :] = a
            cross[term, pl.ds(first, chunk), :] = b
            density = (a * own - b * own_turned).astype(jnp.bfloat16)
            both = jnp.dot(density, forward[...], preferred_element_type=jnp.float32)
            both = both.astype(jnp.bfloat16)
            stack[pl.ds(first, chunk), pl.ds(lane, LANES)] = both[:, :LANES]
            stack[pl.ds(rows + first, chunk), pl.ds(lane, LANES)] = both[:, LANES:]

    spectrum = jnp.dot(
        table[...], stack[...], preferred_element_type=jnp.float32
    )
    for term in range(terms):
        lane = term * LANES
        screened = (spectrum[:, lane : lane + LANES] * kern[term // OCC_DEV]).astype(jnp.bfloat16)
        both = jnp.dot(screened, inverse[...], preferred_element_type=jnp.float32)
        both = both.astype(jnp.bfloat16)
        stack[pl.ds(0, rows), pl.ds(lane, LANES)] = both[:, :LANES]
        stack[pl.ds(rows, rows), pl.ds(lane, LANES)] = both[:, LANES:]
    potential = jnp.dot(
        table[...], stack[...], preferred_element_type=jnp.float32
    )
    total = jnp.zeros((rows, LANES), jnp.float32)
    for term in range(terms):
        lane = term * LANES
        pot = potential[:, lane : lane + LANES]
        total += direct[term] * pot + cross[term] * pltpu.roll(pot, half, 1)
    out[...] = (prefactor * total).astype(out.dtype)


def apply_exchange(visitors, psi, kern, grid_x, grid_y, grid_z):
    rows = grid_y * grid_z
    terms = STEPS * OCC_DEV
    vmem = pl.BlockSpec(memory_space=pltpu.VMEM)
    return pl.pallas_call(
        exchange_kernel,
        out_shape=jax.ShapeDtypeStruct((rows, LANES), jnp.bfloat16),
        in_specs=[vmem] * 6,
        out_specs=vmem,
        scratch_shapes=[
            pltpu.VMEM((terms, rows, LANES), jnp.float32),
            pltpu.VMEM((terms, rows, LANES), jnp.float32),
            pltpu.VMEM((2 * rows, terms * LANES), jnp.bfloat16),
        ],
        compiler_params=pltpu.CompilerParams(vmem_limit_bytes=40 * 1024 * 1024),
    )(
        visitors,
        psi,
        jnp.asarray(plane_table(grid_y, grid_z)),
        jnp.asarray(line_table(grid_x, 1.0)),
        jnp.asarray(line_table(grid_x, -1.0)),
        kern,
    )


def exchange(targets, occupied, wavevectors, umklapp, owners):
    resident = targets[0, 0]
    grid_y, grid_z, last_width = resident.shape
    grid_x = last_width // 2
    rows = grid_y * grid_z
    band = lax.axis_index("band")
    core, slot = band % 2, band // 16
    along_yz, cores = band_groups()
    n_yz = len(cores)

    flat = occupied[0].reshape(n_yz, OCC_DEV * rows // n_yz, last_width)
    spread = lax.all_to_all(flat, "band", 0, 0, tiled=True, axis_index_groups=along_yz)
    spread = lax.all_gather(spread, "band", axis_index_groups=cores)

    wanted = shift_ka_by_core(owners[0], -1)
    owner = lax.dynamic_slice(wanted, (core, slot), (1, 1))[0, 0]
    spread = spread.reshape((2 * n_yz,) + flat.shape[1:])
    chosen = lax.dynamic_index_in_dim(spread, owner % 2 * n_yz + owner // 2, 0, keepdims=False)
    mine = shift_ka_by_core(chosen, 1)

    column = jnp.broadcast_to(mine[None], (n_yz,) + mine.shape)
    column = lax.all_to_all(column, "band", 0, 0, tiled=True, axis_index_groups=along_yz)
    kern = coulomb(wavevectors, umklapp, grid_x, grid_y, grid_z)
    visitors = lax.all_gather(column, "band", axis_index_groups=cores)
    visitors = visitors.reshape(STEPS * OCC_DEV, rows, last_width)

    result = apply_exchange(
        visitors,
        resident.reshape(rows, last_width),
        kern.reshape(STEPS, rows, last_width),
        grid_x,
        grid_y,
        grid_z,
    )
    return result.reshape((1, 1) + resident.shape)


def solution(mesh):
    placed = (
        P("ka", "band", None, None, None),
        P("ka", "band", None, None, None),
        P(),
        P("ka", None, None),
        P("ka", None, None),
    )
    return jax.shard_map(
        exchange,
        mesh=mesh,
        in_specs=placed,
        out_specs=P("ka", "band", None, None, None),
        check_vma=False,
    )
```

time: 78.6 us -> 63.2 us (0.80)
  other arithmetic: 4.72 us -> 0 us
  starting transfers between devices: 34.7 us -> 31.3 us
  blocking collectives: 10.9 us -> 8.13 us
  local copies, waits for them, and re-layouts: 5.61 us -> 3.1 us
  waiting for transfers between devices: 14.4 us -> 12.1 us
  Pallas kernels: 3.49 us -> 5.29 us
  between operations: 4.23 us -> 2.72 us
    ppermute x4 -> x2, starting transfers between devices: 17.6 us -> 11.2 us  [shift_ka_by_core(): return lax.ppermute(block, ('ka', 'band'), route)]
    mul x8 -> x0, other arithmetic: 4.28 us -> none  [the longest x6 3.98 us: coulomb(): squares.append(wavenumber * wavenumber)]
    all_to_all x2, waiting for transfers between devices: 9.6 us -> 5.87 us  [the longest x1 5.87 us: exchange(): lax.all_to_all(column, 'band', 0, 0, tiled=True, axis_index_groups=along_yz)]
    all_to_all x2, starting transfers between devices: 17.1 us -> 20.1 us  [the longest x1 12.1 us: exchange(): lax.all_to_all(flat, 'band', 0, 0, tiled=True, axis_index_groups=along_yz)]
    all_gather x1 -> x2, blocking collectives: 10.9 us -> 8.13 us  [the longest x1 4.73 us: exchange(): visitors = lax.all_gather(column, 'band', axis_index_groups=cores)]
    pallas_call x0 -> x1, Pallas kernels: none -> 1.74 us  [coulomb(): pl.pallas_call(coulomb_kernel, out_shape=jax.ShapeDtypeStruct((STEPS, gri...]
    unnamed x12 -> x13, local copies, waits for them, and re-layouts: 0.02 us -> 1.76 us
    pad x1 -> x0, local copies, waits for them, and re-layouts: 1.72 us -> none  [local(): flat = jnp.pad(flat, ((0, 0), (0, PIECE * PIECES - rows), (0, 0)))]
  transfers between devices with their start and end apart: 6 -> 4, of which waited for: 4 -> 3; matrix products, arithmetic and copies ran while one was open for 11% -> 2% of each run, Pallas kernels for 0% -> 3%
where the time goes in v2:
time: 63.2 us; the launch traced here: 62.7 us
  starting transfers between devices  31.3 us (50%)
  waiting for transfers between devices  12.1 us (19%)
  blocking collectives  8.13 us (13%)
  Pallas kernels  5.29 us (8%)
  local copies, waits for them, and re-layouts  3.1 us (5%)
  between operations  2.72 us (4%)
    all_to_all x1, starting transfers between devices, exchange(): lax.all_to_all(flat, 'band', 0, 0, tiled=True, axis_index_groups=along_yz)  12.1 us
    ppermute x2, starting transfers between devices, shift_ka_by_core(): return lax.ppermute(block, ('ka', 'band'), route)  11.2 us
    all_to_all x1, starting transfers between devices, exchange(): lax.all_to_all(column, 'band', 0, 0, tiled=True, axis_index_groups=along_yz)  8.02 us
    ppermute x2, waiting for transfers between devices, shift_ka_by_core(): return lax.ppermute(block, ('ka', 'band'), route)  6.28 us
    all_to_all x1, waiting for transfers between devices, exchange(): lax.all_to_all(column, 'band', 0, 0, tiled=True, axis_index_groups=along_yz)  5.87 us
    all_gather x1, blocking collectives, exchange(): visitors = lax.all_gather(column, 'band', axis_index_groups=cores)  4.73 us
    pallas_call x1, Pallas kernels, apply_exchange(): pl.pallas_call(exchange_kernel, out_shape=jax.ShapeDtypeStruct((rows, LAN...  3.55 us
    all_gather x1, blocking collectives, exchange(): spread = lax.all_gather(spread, 'band', axis_index_groups=cores)  3.4 us
  transfers between devices with their start and end apart: 4, of which 3 were waited for; matrix products, arithmetic and copies ran while one was open for 2% of the time, Pallas kernels for 3%

profile of v2, /device:TPU:1, one launch (start us, length us, event | category | flops | bytes accessed | tf_op | source)
XLA Modules:
  0.0 62.7 jit_solution(5113259157247140277)
XLA Ops:
  0.0 0.0 copy-start.5
  0.0 12.1 %all-to-all-start = ((bf16[16,72,128]{2,1,0:T(8,128)(2,1)}), bf16[16,72,128]{2,1,0:T(8,128)(2,1)S(1)}, u32[]{:S(2)}, u32[]{:S(2)}) async-start(bf16[16,72,128]{2,1,0:T(8,128)(2,1)} %bitcast.12), calls=%async_computation | async-start | bytes 589824 | tf_op jit(solution)/shard_map/all_to_all | solution.py:184
  12.1 7.4 %collective-permute-start = (s32[2,2]{1,0:T(2,128)}, s32[2,2]{1,0:T(2,128)S(1)}, u32[]{:S(2)}, u32[]{:S(2)}) collective-permute-start(s32[2,2]{1,0:T(2,128)} %bitcast.13), channel_id=1, source_target_pairs={{0,480},{1,449},{2,482},{3,451},{4,484},{5,453},{6,486},{7,455},{8... | collective-permute-start | bytes 56 | tf_op jit(solution)/shard_map/ppermute | solution.py:31
  19.6 0.9 %collective-permute-done = s32[2,2]{1,0:T(2,128)S(1)} collective-permute-done((s32[2,2]{1,0:T(2,128)}, s32[2,2]{1,0:T(2,128)S(1)}, u32[]{:S(2)}, u32[]{:S(2)}) %collective-permute-start) | collective-permute-done | bytes 48 | tf_op jit(solution)/shard_map/ppermute | solution.py:31
  20.5 0.6 dynamic_slice.7
  23.7 0.0 all-to-all-done
  23.7 3.4 %all-gather = bf16[32,72,128]{2,1,0:T(8,128)(2,1)S(1)} all-gather(bf16[16,72,128]{2,1,0:T(8,128)(2,1)S(1)} %all-to-all-done), channel_id=2, replica_groups={{0,1},{2,3},{4,5},{6,7},{8,9},{10,11},{12,13},{14,15},{16,17},{18,19},{..., dimensions={0}, use_global_device_ids=true | all-gather | bytes 884736 | tf_op jit(solution)/shard_map/all_gather | solution.py:185
  27.1 0.0 copy-start.1
  27.1 0.0 copy-start.2
  27.1 0.0 copy-start.3
  27.1 0.0 copy-start.4
  27.1 3.8 %collective-permute-start.1 = (bf16[72,128]{1,0:T(8,128)(2,1)S(1)}, bf16[72,128]{1,0:T(8,128)(2,1)S(1)}, u32[]{:S(2)}, u32[]{:S(2)}) collective-permute-start(bf16[72,128]{1,0:T(8,128)(2,1)S(1)} %dynamic-slice_bitcast_fusion), channel_id=1, source_target_pairs={{0,32},{1,65},{2,34},{3,67},{4,36},{5,69},{6,38},{7,71},{8,40},{9,... | collective-permute-start | bytes 55304 | tf_op jit(solution)/shard_map/ppermute | solution.py:31
  30.9 5.4 %collective-permute-done.1 = bf16[72,128]{1,0:T(8,128)(2,1)S(1)} collective-permute-done((bf16[72,128]{1,0:T(8,128)(2,1)S(1)}, bf16[72,128]{1,0:T(8,128)(2,1)S(1)}, u32[]{:S(2)}, u32[]{:S(2)}) %collective-permute-start.1) | collective-permute-done | bytes 18464 | tf_op jit(solution)/shard_map/ppermute | solution.py:31
  36.3 0.8 %broadcast_in_dim.2 = bf16[16,72,128]{2,1,0:T(8,128)(2,1)} broadcast(bf16[72,128]{1,0:T(8,128)(2,1)S(1)} %collective-permute-done.1), dimensions={1,2} | broadcast | bytes 313344 | tf_op jit(solution)/shard_map/broadcast_in_dim | solution.py:193
  37.0 8.0 %all-to-all-start.1 = ((bf16[16,72,128]{2,1,0:T(8,128)(2,1)}), bf16[16,72,128]{2,1,0:T(8,128)(2,1)S(1)}, u32[]{:S(2)}, u32[]{:S(2)}) async-start(bf16[16,72,128]{2,1,0:T(8,128)(2,1)} %broadcast_in_dim.2), calls=%async_computation.1 | async-start | bytes 589824 | tf_op jit(solution)/shard_map/all_to_all | solution.py:194
  45.0 0.0 copy-done.5
  45.0 0.7 %copy.10.wavevectors = s32[16,3]{1,0:T(8,128)} copy(s32[16,3]{0,1:T(4,128)S(1)} %copy-done.5) | data formatting | bytes 384 | tf_op args[2]
  45.7 1.7 %shard_map.82 = f32[2,24,24,128]{3,2,1,0:T(8,128)} custom-call(s32[16,3]{1,0:T(8,128)} %copy.10.wavevectors, s32[1,2,3]{2,1,0:T(2,128)} %umklapp.1), custom_call_target="tpu_custom_call" | custom-call | tf_op jit(solution)/shard_map/pallas_call | solution.py:96
  47.5 5.9 %all-to-all-done.1 = bf16[16,72,128]{2,1,0:T(8,128)(2,1)S(1)} async-done(((bf16[16,72,128]{2,1,0:T(8,128)(2,1)}), bf16[16,72,128]{2,1,0:T(8,128)(2,1)S(1)}, u32[]{:S(2)}, u32[]{:S(2)}) %all-to-all-start.1) | async-done | bytes 294944 | tf_op jit(solution)/shard_map/all_to_all | solution.py:194
  53.3 4.7 %all-gather.1 = bf16[32,72,128]{2,1,0:T(8,128)(2,1)S(1)} all-gather(bf16[16,72,128]{2,1,0:T(8,128)(2,1)S(1)} %all-to-all-done.1), channel_id=3, replica_groups={{0,1},{2,3},{4,5},{6,7},{8,9},{10,11},{12,13},{14,15},{16,17},{18,19},{..., dimensions={0}, use_global_device_ids=true | all-gather | bytes 884736 | tf_op jit(solution)/shard_map/all_gather | solution.py:196
  58.1 0.0 copy-done.1
  58.1 0.0 copy-done.2
  58.1 0.0 copy-done.3
  58.1 0.0 copy-done.4
  58.1 0.0 copy-start
  58.1 1.1 %copy-done = f32[2,24,24,128]{3,2,1,0:T(8,128)S(1)} copy-done((f32[2,24,24,128]{3,2,1,0:T(8,128)S(1)}, f32[2,24,24,128]{3,2,1,0:T(8,128)}, u32[]{:S(2)}) %copy-start) | copy-done | bytes 589848
  59.2 3.6 %shard_map.83 = bf16[576,128]{1,0:T(8,128)(2,1)} custom-call(bf16[4,576,128]{2,1,0:T(8,128)(2,1)S(1)} %bitcast.10, bf16[576,128]{1,0:T(8,128)(2,1)S(1)} %bitcast.11, bf16[576,1152]{1,0:T(8,128)(2,1)S(1)} %copy-done.1, bf16[128,256]{1,0:T(8,128)(2,1)S(1)} %copy-done.4, bf16[128,256]{1,0:T(8,128)(2,1)S(1)} %copy-done.3, f32[2,576,128]{2,1,0:T(8,128)S(1)} %bitcast.9), custom_call_target="tpu_custom_call" | custom-call | tf_op jit(solution)/shard_map/pallas_call | solution.py:152
  (1 shorter events, 0.0 us)
Async XLA Ops:
  0.0 45.0 %copy-start.5 = (s32[16,3]{0,1:T(4,128)S(1)}, s32[16,3]{0,1:T(4,128)}, u32[]{:S(2)}) copy-start(s32[16,3]{0,1:T(4,128)} %param.10) | copy-start | bytes 580
  0.0 23.7 %all-to-all-start = ((bf16[16,72,128]{2,1,0:T(8,128)(2,1)}), bf16[16,72,128]{2,1,0:T(8,128)(2,1)S(1)}, u32[]{:S(2)}, u32[]{:S(2)}) async-start(bf16[16,72,128]{2,1,0:T(8,128)(2,1)} %bitcast.12), calls=%async_computation | async-start | bytes 589824 | tf_op jit(solution)/shard_map/all_to_all | solution.py:184
  12.1 8.4 %collective-permute-start = (s32[2,2]{1,0:T(2,128)}, s32[2,2]{1,0:T(2,128)S(1)}, u32[]{:S(2)}, u32[]{:S(2)}) collective-permute-start(s32[2,2]{1,0:T(2,128)} %bitcast.13), channel_id=1, source_target_pairs={{0,480},{1,449},{2,482},{3,451},{4,484},{5,453},{6,486},{7,455},{8... | collective-permute-start | bytes 56 | tf_op jit(solution)/shard_map/ppermute | solution.py:31
  27.1 31.0 %copy-start.1 = (bf16[576,1152]{1,0:T(8,128)(2,1)S(1)}, bf16[576,1152]{1,0:T(8,128)(2,1)}, u32[]{:S(2)}) copy-start(bf16[576,1152]{1,0:T(8,128)(2,1)} %constant.56.clone.table) | copy-start | bytes 3981316
  27.1 31.0 %copy-start.2 = (bf16[1,1,24,24,128]{4,3,2,1,0:T(8,128)(2,1)S(1)}, bf16[1,1,24,24,128]{4,3,2,1,0:T(8,128)(2,1)}, u32[]{:S(2)}) copy-start(bf16[1,1,24,24,128]{4,3,2,1,0:T(8,128)(2,1)} %param.8) | copy-start | bytes 442372
  27.1 31.0 %copy-start.3 = (bf16[128,256]{1,0:T(8,128)(2,1)S(1)}, bf16[128,256]{1,0:T(8,128)(2,1)}, u32[]{:S(2)}) copy-start(bf16[128,256]{1,0:T(8,128)(2,1)} %constant.58.clone.inverse) | copy-start | bytes 196612
  27.1 31.0 %copy-start.4 = (bf16[128,256]{1,0:T(8,128)(2,1)S(1)}, bf16[128,256]{1,0:T(8,128)(2,1)}, u32[]{:S(2)}) copy-start(bf16[128,256]{1,0:T(8,128)(2,1)} %constant.57.clone.forward) | copy-start | bytes 196612
  27.1 9.1 %collective-permute-start.1 = (bf16[72,128]{1,0:T(8,128)(2,1)S(1)}, bf16[72,128]{1,0:T(8,128)(2,1)S(1)}, u32[]{:S(2)}, u32[]{:S(2)}) collective-permute-start(bf16[72,128]{1,0:T(8,128)(2,1)S(1)} %dynamic-slice_bitcast_fusion), channel_id=1, source_target_pairs={{0,32},{1,65},{2,34},{3,67},{4,36},{5,69},{6,38},{7,71},{8,40},{9,... | collective-permute-start | bytes 55304 | tf_op jit(solution)/shard_map/ppermute | solution.py:31
  37.0 16.3 %all-to-all-start.1 = ((bf16[16,72,128]{2,1,0:T(8,128)(2,1)}), bf16[16,72,128]{2,1,0:T(8,128)(2,1)S(1)}, u32[]{:S(2)}, u32[]{:S(2)}) async-start(bf16[16,72,128]{2,1,0:T(8,128)(2,1)} %broadcast_in_dim.2), calls=%async_computation.1 | async-start | bytes 589824 | tf_op jit(solution)/shard_map/all_to_all | solution.py:194
  58.1 1.1 %copy-start = (f32[2,24,24,128]{3,2,1,0:T(8,128)S(1)}, f32[2,24,24,128]{3,2,1,0:T(8,128)}, u32[]{:S(2)}) copy-start(f32[2,24,24,128]{3,2,1,0:T(8,128)} %shard_map.82) | copy-start | bytes 1769476

commit v3 on v2

--- a/solution.py
+++ b/solution.py
@@ -79,7 +79,7 @@
     for s in range(steps):
         visit = lax.rem(k + (k_total - s - 1), k_total)
         shift = [
-            (wavevectors[k, a] - wavevectors[visit, a]).astype(jnp.float32) / KGRID
+            (wavevectors[a, k] - wavevectors[a, visit]).astype(jnp.float32) / KGRID
             + umklapp[0, s, a].astype(jnp.float32)
             for a in range(3)
         ]
@@ -98,7 +98,7 @@
         out_shape=jax.ShapeDtypeStruct((STEPS, grid_y, grid_z, 2 * grid_x), jnp.float32),
         in_specs=[smem, smem],
         out_specs=pl.BlockSpec(memory_space=pltpu.VMEM),
-    )(wavevectors, umklapp)
+    )(wavevectors.T, umklapp)
 
 
 def exchange_kernel(visitors, psi, table, forward, inverse, kern, out, direct, cross, stack):
@@ -185,14 +185,17 @@
     spread = lax.all_gather(spread, "band", axis_index_groups=cores)
 
     wanted = shift_ka_by_core(owners[0], -1)
-    owner = lax.dynamic_slice(wanted, (core, slot), (1, 1))[0, 0]
+    kern = coulomb(wavevectors, umklapp, grid_x, grid_y, grid_z)
+    owner = lax.dynamic_slice(wanted, (core, slot), (1, 1), allow_negative_indices=False)[0, 0]
     spread = spread.reshape((2 * n_yz,) + flat.shape[1:])
-    chosen = lax.dynamic_index_in_dim(spread, owner % 2 * n_yz + owner // 2, 0, keepdims=False)
+    place = jnp.bitwise_and(owner, 1) * n_yz + lax.shift_right_logical(owner, 1)
+    chosen = lax.dynamic_slice(
+        spread, (place, 0, 0), (1,) + flat.shape[1:], allow_negative_indices=False
+    )[0]
     mine = shift_ka_by_core(chosen, 1)
 
     column = jnp.broadcast_to(mine[None], (n_yz,) + mine.shape)
     column = lax.all_to_all(column, "band", 0, 0, tiled=True, axis_index_groups=along_yz)
-    kern = coulomb(wavevectors, umklapp, grid_x, grid_y, grid_z)
     visitors = lax.all_gather(column, "band", axis_index_groups=cores)
     visitors = visitors.reshape(STEPS * OCC_DEV, rows, last_width)
 

time: 63.2 us -> 61.7 us (0.976)
  between operations: 2.72 us -> 1.39 us
  local copies, waits for them, and re-layouts: 3.1 us -> 2.42 us
    ppermute x2, starting transfers between devices: 11.2 us -> 12.2 us  [shift_ka_by_core(): return lax.ppermute(block, ('ka', 'band'), route)]
    ppermute x2, waiting for transfers between devices: 6.28 us -> 5.25 us  [shift_ka_by_core(): return lax.ppermute(block, ('ka', 'band'), route)]
    all_to_all x1, waiting for transfers between devices: 5.87 us -> 6.65 us  [exchange(): lax.all_to_all(column, 'band', 0, 0, tiled=True, axis_index_groups=along_yz)]
    unnamed x13 -> x10, local copies, waits for them, and re-layouts: 1.76 us -> 1.07 us
  transfers between devices with their start and end apart: 4 -> 4, of which waited for: 3 -> 3; matrix products, arithmetic and copies ran while one was open for 2% -> 1% of each run, Pallas kernels for 3% -> 3%
where the time goes in v3:
time: 61.7 us; the launch traced here: 61.3 us
  starting transfers between devices  31.9 us (52%)
  waiting for transfers between devices  11.9 us (19%)
  blocking collectives  8.42 us (14%)
  Pallas kernels  5.2 us (8%)
  local copies, waits for them, and re-layouts  2.42 us (4%)
  between operations  1.39 us (2%)
    ppermute x2, starting transfers between devices, shift_ka_by_core(): return lax.ppermute(block, ('ka', 'band'), route)  12.2 us
    all_to_all x1, starting transfers between devices, exchange(): lax.all_to_all(flat, 'band', 0, 0, tiled=True, axis_index_groups=along_yz)  12 us
    all_to_all x1, starting transfers between devices, exchange(): lax.all_to_all(column, 'band', 0, 0, tiled=True, axis_index_groups=along_yz)  7.73 us
    all_to_all x1, waiting for transfers between devices, exchange(): lax.all_to_all(column, 'band', 0, 0, tiled=True, axis_index_groups=along_yz)  6.65 us
    ppermute x2, waiting for transfers between devices, shift_ka_by_core(): return lax.ppermute(block, ('ka', 'band'), route)  5.25 us
    all_gather x1, blocking collectives, exchange(): visitors = lax.all_gather(column, 'band', axis_index_groups=cores)  4.73 us
    all_gather x1, blocking collectives, exchange(): spread = lax.all_gather(spread, 'band', axis_index_groups=cores)  3.68 us
    pallas_call x1, Pallas kernels, apply_exchange(): pl.pallas_call(exchange_kernel, out_shape=jax.ShapeDtypeStruct((rows, LAN...  3.55 us
  transfers between devices with their start and end apart: 4, of which 3 were waited for; matrix products, arithmetic and copies ran while one was open for 1% of the time, Pallas kernels for 3%

profile of v3, /device:TPU:1, one launch (start us, length us, event | category | flops | bytes accessed | tf_op | source)
XLA Modules:
  0.0 61.3 jit_solution(519282548557193)
XLA Ops:
  0.0 12.0 %all-to-all-start = ((bf16[16,72,128]{2,1,0:T(8,128)(2,1)}), bf16[16,72,128]{2,1,0:T(8,128)(2,1)S(1)}, u32[]{:S(2)}, u32[]{:S(2)}) async-start(bf16[16,72,128]{2,1,0:T(8,128)(2,1)} %bitcast.13), calls=%async_computation | async-start | bytes 589824 | tf_op jit(solution)/shard_map/all_to_all | solution.py:184
  12.0 7.4 %collective-permute-start = (s32[2,2]{1,0:T(2,128)}, s32[2,2]{1,0:T(2,128)S(1)}, u32[]{:S(2)}, u32[]{:S(2)}) collective-permute-start(s32[2,2]{1,0:T(2,128)} %bitcast.15), channel_id=1, source_target_pairs={{0,480},{1,449},{2,482},{3,451},{4,484},{5,453},{6,486},{7,455},{8... | collective-permute-start | bytes 56 | tf_op jit(solution)/shard_map/ppermute | solution.py:31
  19.5 0.9 %collective-permute-done = s32[2,2]{1,0:T(2,128)S(1)} collective-permute-done((s32[2,2]{1,0:T(2,128)}, s32[2,2]{1,0:T(2,128)S(1)}, u32[]{:S(2)}, u32[]{:S(2)}) %collective-permute-start) | collective-permute-done | bytes 48 | tf_op jit(solution)/shard_map/ppermute | solution.py:31
  20.3 0.6 dynamic_slice.6
  22.2 0.0 all-to-all-done
  22.2 3.7 %all-gather = bf16[32,72,128]{2,1,0:T(8,128)(2,1)S(1)} all-gather(bf16[16,72,128]{2,1,0:T(8,128)(2,1)S(1)} %all-to-all-done), channel_id=2, replica_groups={{0,1},{2,3},{4,5},{6,7},{8,9},{10,11},{12,13},{14,15},{16,17},{18,19},{..., dimensions={0}, use_global_device_ids=true | all-gather | bytes 884736 | tf_op jit(solution)/shard_map/all_gather | solution.py:185
  25.9 0.0 copy-start.1
  25.9 0.0 copy-start.2
  25.9 0.0 copy-start.3
  25.9 0.0 copy-start.4
  25.9 4.8 %collective-permute-start.1 = (bf16[72,128]{1,0:T(8,128)(2,1)S(1)}, bf16[72,128]{1,0:T(8,128)(2,1)S(1)}, u32[]{:S(2)}, u32[]{:S(2)}) collective-permute-start(bf16[72,128]{1,0:T(8,128)(2,1)S(1)} %dynamic-slice_bitcast_fusion), channel_id=1, source_target_pairs={{0,32},{1,65},{2,34},{3,67},{4,36},{5,69},{6,38},{7,71},{8,40},{9,... | collective-permute-start | bytes 55304 | tf_op jit(solution)/shard_map/ppermute | solution.py:31
  30.7 4.4 %collective-permute-done.1 = bf16[72,128]{1,0:T(8,128)(2,1)S(1)} collective-permute-done((bf16[72,128]{1,0:T(8,128)(2,1)S(1)}, bf16[72,128]{1,0:T(8,128)(2,1)S(1)}, u32[]{:S(2)}, u32[]{:S(2)}) %collective-permute-start.1) | collective-permute-done | bytes 18464 | tf_op jit(solution)/shard_map/ppermute | solution.py:31
  35.1 0.8 %broadcast_in_dim.2 = bf16[16,72,128]{2,1,0:T(8,128)(2,1)} broadcast(bf16[72,128]{1,0:T(8,128)(2,1)S(1)} %collective-permute-done.1), dimensions={1,2} | broadcast | bytes 313344 | tf_op jit(solution)/shard_map/broadcast_in_dim | solution.py:197
  35.9 7.7 %all-to-all-start.1 = ((bf16[16,72,128]{2,1,0:T(8,128)(2,1)}), bf16[16,72,128]{2,1,0:T(8,128)(2,1)S(1)}, u32[]{:S(2)}, u32[]{:S(2)}) async-start(bf16[16,72,128]{2,1,0:T(8,128)(2,1)} %broadcast_in_dim.2), calls=%async_computation.1 | async-start | bytes 589824 | tf_op jit(solution)/shard_map/all_to_all | solution.py:198
  43.6 1.6 %shard_map.82 = f32[2,24,24,128]{3,2,1,0:T(8,128)} custom-call(s32[3,16]{1,0:T(4,128)} %bitcast.14, s32[1,2,3]{2,1,0:T(2,128)} %umklapp.1), custom_call_target="tpu_custom_call" | custom-call | tf_op jit(solution)/shard_map/pallas_call | solution.py:96
  45.2 6.7 %all-to-all-done.1 = bf16[16,72,128]{2,1,0:T(8,128)(2,1)S(1)} async-done(((bf16[16,72,128]{2,1,0:T(8,128)(2,1)}), bf16[16,72,128]{2,1,0:T(8,128)(2,1)S(1)}, u32[]{:S(2)}, u32[]{:S(2)}) %all-to-all-start.1) | async-done | bytes 294944 | tf_op jit(solution)/shard_map/all_to_all | solution.py:198
  51.9 4.7 %all-gather.1 = bf16[32,72,128]{2,1,0:T(8,128)(2,1)S(1)} all-gather(bf16[16,72,128]{2,1,0:T(8,128)(2,1)S(1)} %all-to-all-done.1), channel_id=3, replica_groups={{0,1},{2,3},{4,5},{6,7},{8,9},{10,11},{12,13},{14,15},{16,17},{18,19},{..., dimensions={0}, use_global_device_ids=true | all-gather | bytes 884736 | tf_op jit(solution)/shard_map/all_gather | solution.py:199
  56.6 0.0 copy-done.1
  56.6 0.0 copy-done.2
  56.6 0.0 copy-done.3
  56.6 0.0 copy-done.4
  56.6 0.0 copy-start
  56.7 1.1 %copy-done = f32[2,24,24,128]{3,2,1,0:T(8,128)S(1)} copy-done((f32[2,24,24,128]{3,2,1,0:T(8,128)S(1)}, f32[2,24,24,128]{3,2,1,0:T(8,128)}, u32[]{:S(2)}) %copy-start) | copy-done | bytes 589848
  57.7 3.6 %shard_map.83 = bf16[576,128]{1,0:T(8,128)(2,1)} custom-call(bf16[4,576,128]{2,1,0:T(8,128)(2,1)S(1)} %bitcast.11, bf16[576,128]{1,0:T(8,128)(2,1)S(1)} %bitcast.12, bf16[576,1152]{1,0:T(8,128)(2,1)S(1)} %copy-done.1, bf16[128,256]{1,0:T(8,128)(2,1)S(1)} %copy-done.4, bf16[128,256]{1,0:T(8,128)(2,1)S(1)} %copy-done.3, f32[2,576,128]{2,1,0:T(8,128)S(1)} %bitcast.10), custom_call_target="tpu_custom_call" | custom-call | tf_op jit(solution)/shard_map/pallas_call | solution.py:152
  (1 shorter events, 0.0 us)
Async XLA Ops:
  0.0 22.2 %all-to-all-start = ((bf16[16,72,128]{2,1,0:T(8,128)(2,1)}), bf16[16,72,128]{2,1,0:T(8,128)(2,1)S(1)}, u32[]{:S(2)}, u32[]{:S(2)}) async-start(bf16[16,72,128]{2,1,0:T(8,128)(2,1)} %bitcast.13), calls=%async_computation | async-start | bytes 589824 | tf_op jit(solution)/shard_map/all_to_all | solution.py:184
  12.0 8.4 %collective-permute-start = (s32[2,2]{1,0:T(2,128)}, s32[2,2]{1,0:T(2,128)S(1)}, u32[]{:S(2)}, u32[]{:S(2)}) collective-permute-start(s32[2,2]{1,0:T(2,128)} %bitcast.15), channel_id=1, source_target_pairs={{0,480},{1,449},{2,482},{3,451},{4,484},{5,453},{6,486},{7,455},{8... | collective-permute-start | bytes 56 | tf_op jit(solution)/shard_map/ppermute | solution.py:31
  25.9 30.7 %copy-start.1 = (bf16[576,1152]{1,0:T(8,128)(2,1)S(1)}, bf16[576,1152]{1,0:T(8,128)(2,1)}, u32[]{:S(2)}) copy-start(bf16[576,1152]{1,0:T(8,128)(2,1)} %constant.44.clone.table) | copy-start | bytes 3981316
  25.9 30.7 %copy-start.2 = (bf16[1,1,24,24,128]{4,3,2,1,0:T(8,128)(2,1)S(1)}, bf16[1,1,24,24,128]{4,3,2,1,0:T(8,128)(2,1)}, u32[]{:S(2)}) copy-start(bf16[1,1,24,24,128]{4,3,2,1,0:T(8,128)(2,1)} %param.8) | copy-start | bytes 442372
  25.9 30.7 %copy-start.3 = (bf16[128,256]{1,0:T(8,128)(2,1)S(1)}, bf16[128,256]{1,0:T(8,128)(2,1)}, u32[]{:S(2)}) copy-start(bf16[128,256]{1,0:T(8,128)(2,1)} %constant.46.clone.inverse) | copy-start | bytes 196612
  25.9 30.7 %copy-start.4 = (bf16[128,256]{1,0:T(8,128)(2,1)S(1)}, bf16[128,256]{1,0:T(8,128)(2,1)}, u32[]{:S(2)}) copy-start(bf16[128,256]{1,0:T(8,128)(2,1)} %constant.45.clone.forward) | copy-start | bytes 196612
  25.9 9.1 %collective-permute-start.1 = (bf16[72,128]{1,0:T(8,128)(2,1)S(1)}, bf16[72,128]{1,0:T(8,128)(2,1)S(1)}, u32[]{:S(2)}, u32[]{:S(2)}) collective-permute-start(bf16[72,128]{1,0:T(8,128)(2,1)S(1)} %dynamic-slice_bitcast_fusion), channel_id=1, source_target_pairs={{0,32},{1,65},{2,34},{3,67},{4,36},{5,69},{6,38},{7,71},{8,40},{9,... | collective-permute-start | bytes 55304 | tf_op jit(solution)/shard_map/ppermute | solution.py:31
  35.9 16.0 %all-to-all-start.1 = ((bf16[16,72,128]{2,1,0:T(8,128)(2,1)}), bf16[16,72,128]{2,1,0:T(8,128)(2,1)S(1)}, u32[]{:S(2)}, u32[]{:S(2)}) async-start(bf16[16,72,128]{2,1,0:T(8,128)(2,1)} %broadcast_in_dim.2), calls=%async_computation.1 | async-start | bytes 589824 | tf_op jit(solution)/shard_map/all_to_all | solution.py:198
  56.6 1.1 %copy-start = (f32[2,24,24,128]{3,2,1,0:T(8,128)S(1)}, f32[2,24,24,128]{3,2,1,0:T(8,128)}, u32[]{:S(2)}) copy-start(f32[2,24,24,128]{3,2,1,0:T(8,128)} %shard_map.82) | copy-start | bytes 1769476
